TPU v7x, 32 devices: a 4x4x1 block of a 4x4x8 slice. The times are simulated.
32 devices in a mesh: dp: 2 (over z, core), sp: 16 (over x, y).
Axes of the slice: x: 4, y: 4, z: 1, core: 2. Of those that a mesh axis runs over, the one named last changes fastest.
The devices are a block of a 4x4x8 slice.
Arguments:
- q: bfloat16 [64, 8, 256], P('dp'), parts along dimension 0
- k: bfloat16 [64, 8192, 8, 256], P('dp', 'sp'), parts along dimension 0
- v: bfloat16 [64, 8192, 8, 256], P('dp', 'sp'), parts along dimension 0
Outputs:
- q: bfloat16 [64, 8, 256], P('dp'), parts along dimension 0
There are 2 independent parts. A program takes and returns all parts, laid end to end along the dimension named above; each array names one.
All inputs are finite; a program needn't handle non-finite values.
Results may differ from a plain program's by a relative error of at most 0.012.
Values are sent between devices in bfloat16 or wider.
A program may use at most 768 MiB of HBM per device.

v0:
```python
import jax
import jax.numpy as jnp
from jax import lax
from jax.sharding import PartitionSpec as P


def einsum(form, a, b):
    return jnp.einsum(form, a.astype(jnp.float32), b.astype(jnp.float32))


def part_of(q, k, v):
    grouped = q.reshape(q.shape[0], k.shape[2], -1, q.shape[2])
    scores = einsum("bgsd,bugd->bgsu", grouped, k) * q.shape[2] ** -0.5
    high = jnp.max(scores, -1, keepdims=True)
    weights = jnp.exp(scores - high)
    seen = einsum("bgsu,bugd->bgsd", weights.astype(jnp.bfloat16), v)
    return jnp.concatenate([seen, jnp.sum(weights, -1, keepdims=True), high], -1)


def together(parts):
    seen, total, high = parts[..., :-2], parts[..., -2:-1], parts[..., -1:]
    scale = jnp.exp(high - jnp.max(high, 0))
    return (jnp.sum(seen * scale, 0) / jnp.sum(total * scale, 0)).astype(jnp.bfloat16)


def solution(mesh):
    def step(q, k, v):
        return together(lax.all_gather(part_of(q, k, v), "sp")).reshape(q.shape)

    return jax.shard_map(
        step,
        mesh=mesh,
        in_specs=(P("dp", None, None), P("dp", "sp", None, None), P("dp", "sp", None, None)),
        out_specs=P("dp", None, None),
        check_vma=False,
    )
```

profile of v0, /device:TPU:97, one launch (start us, length us, event | category | flops | bytes accessed | tf_op | source)
XLA Modules:
  0.0 151.1 jit_solution(4267646093604095733)
XLA Ops:
  6.5 0.0 all-gather.3.cloned.1.call-start
  6.6 31.9 %fusion.2 = f32[32,8,1,512]{3,2,1,0:T(1,128)S(1)} fusion(bf16[32,512,8,256]{3,2,1,0:T(8,128)(2,1)} %param.4, bf16[32,8,256,1]{2,1,0,3:T(8,128)(2,1)} %bitcast.27), kind=kOutput, calls=%fused_computation.2 | convolution fusion | flops 67108864 | bytes 67764224 | tf_op jit(solution)/shard_map/bgsd,bugd->bgsu/dot_general | solution.py:8
  38.4 0.1 fusion.9
  38.5 0.2 fusion.10
  38.8 32.6 %fusion = f32[32,8,1,256]{3,2,1,0:T(1,128)S(1)} fusion(bf16[32,512,8,256]{3,2,1,0:T(8,128)(2,1)} %param.5, bf16[32,8,512,1]{2,1,0,3:T(8,128)(2,1)S(1)} %get-tuple-element.7), kind=kOutput, calls=%fused_computation | convolution fusion | flops 67108864 | bytes 67633152 | tf_op jit(solution)/shard_map/bgsu,bugd->bgsd/dot_general | solution.py:8
  71.5 0.3 copy.23
  71.7 0.3 copy.22
  72.0 0.9 pad_maximum_fusion
  72.9 0.1 all-gather.3.cloned.1.call-update
  72.9 59.5 %all-gather.3.cloned.1.call-done = f32[512,8,1,258]{3,1,2,0:T(8,128)} async-done(((f32[32,8,1,258]{3,1,2,0:T(8,128)}), f32[512,8,1,258]{3,1,2,0:T(8,128)}) %all-gather.3.cloned.1.call-update) | async-done | bytes 4227088 | tf_op jit(solution)/shard_map/all_gather | solution.py:28
  132.5 2.3 %slice_reduce_fusion = f32[32,8]{1,0:T(8,128)S(1)} fusion(f32[16,32,8,1,258]{4,2,1,0,3:T(8,128)} %bitcast.22), kind=kLoop, calls=%fused_computation.9 | loop fusion | flops 3840 | bytes 17408 | tf_op jit(solution)/shard_map/reduce_max | solution.py:22
  134.7 3.0 %fusion.5 = (f32[32,8]{1,0:T(8,128)S(1)}, f32[16,32,8,1,1]{4,2,1,0,3:T(8,128)S(1)}) fusion(f32[16,32,8,1,258]{4,2,1,0,3:T(8,128)} %bitcast.23, f32[32,8]{1,0:T(8,128)S(1)} %slice_reduce_fusion), kind=kLoop, calls=%fused_computation.7 | loop fusion | flops 12032 | bytes 51200 | tf_op jit(solution)/shard_map/reduce_sum | solution.py:23
  137.7 3.1 %copy.36 = f32[16,32,8,1,1]{2,1,0,3,4:T(8,128)S(1)} copy(f32[16,32,8,1,1]{4,2,1,0,3:T(8,128)S(1)} %get-tuple-element.6) | data formatting | bytes 32768 | tf_op jit(solution)/shard_map/mul | solution.py:23
  140.8 2.7 %fusion.4 = f32[32,8,256]{2,1,0:T(8,128)S(1)} fusion(f32[16,32,8,1,258]{4,2,1,0,3:T(8,128)} %bitcast.24, f32[16,32,8]{2,1,0:T(8,128)S(1)} %bitcast.25), kind=kLoop, calls=%fused_computation.5 | loop fusion | flops 2031616 | bytes 4472832 | tf_op jit(solution)/shard_map/reduce_sum | solution.py:23
  143.5 0.8 divide_convert_fusion
  (1 shorter events, 0.0 us)
Async XLA Ops:
  6.5 125.9 %all-gather.3.cloned.1.call-start = ((), (), s32[]{:S(2)}) async-start(), calls=%async_computation | async-start | bytes 6684672 | tf_op jit(solution)/shard_map/all_gather | solution.py:28
Sparse Core Ops, SparseCore 0:
  73.0 59.3 all-gather.2
where the time goes:
time: 151 us
  matrix products  64.5 us (43%)
  waiting for transfers between devices  59.6 us (39%)
  between operations  13.5 us (9%)
  other arithmetic  9.95 us (7%)
  local copies, waits for them, and re-layouts  3.6 us (2%)
    dot_general x2, matrix products, einsum(): return jnp.einsum(form, a.astype(jnp.float32), b.astype(jnp.float32))  64.5 us
    all_gather x1, waiting for transfers between devices, step(): return together(lax.all_gather(part_of(q, k, v), 'sp')).reshape(q.shape)  59.5 us
    mul x1, local copies, waits for them, and re-layouts, together(): seen * scale  3.06 us
  transfers between devices with their start and end apart: 1, of which 1 were waited for; matrix products, arithmetic and copies ran while one was open for 0% of the time, Pallas kernels for 0%

commit v1 on v0

v1 whole, which is shorter than its diff:
```python
import functools
import math

import jax
import jax.numpy as jnp
from jax import lax
from jax.experimental import pallas as pl
from jax.experimental.pallas import tpu as pltpu
from jax.sharding import PartitionSpec as P

SLOTS = 6
CHUNKS = (2, 1, 1)
LANES = 128
AXIS = "sp"
MESH = pl.DeviceIdType.MESH
COLLECTIVE = 0


def offsets(n):
    side = math.isqrt(n)
    near = lambda a: min(a, side - a)
    return sorted(range(1, n), key=lambda o: -(near(o // side % side) + near(o % side)))


def kernel(
    n, seqs, rows, heads, width, scale,
    q_hbm, k_hbm, v_hbm, o_hbm,
    qbuf, kbuf, vbuf, w0, w1, part, stat, out,
    rs_data, rs_stat, dr_data, dr_stat,
    qsem, ksem, vsem, osem,
    rs_send, rs_recv, ag_send, ag_recv, dr_send, dr_recv,
):
    me = lax.axis_index(AXIS)
    direct = sum(CHUNKS)
    ringed = seqs - direct
    starts = [ringed + sum(CHUNKS[:c]) for c in range(len(CHUNKS))]
    order = offsets(n)

    def k_copy(i):
        slot = lax.rem(i, SLOTS)
        return pltpu.make_async_copy(k_hbm.at[i], kbuf.at[slot], ksem.at[slot])

    def v_copy(i):
        slot = lax.rem(i, SLOTS)
        return pltpu.make_async_copy(v_hbm.at[i], vbuf.at[slot], vsem.at[slot])

    q_copy = pltpu.make_async_copy(q_hbm, qbuf, qsem)
    q_copy.start()
    k_copy(0).start()
    for i in range(SLOTS - 1):
        k_copy(i + 1).start()
        v_copy(i).start()

    barrier = pltpu.get_barrier_semaphore()
    for o in order:
        pl.semaphore_signal(barrier, inc=1, device_id={AXIS: lax.rem(me + o, n)}, device_id_type=MESH)
    pl.semaphore_wait(barrier, n - 1)

    lane = lax.broadcasted_iota(jnp.int32, (heads, LANES), 1)
    sub = lax.broadcasted_iota(jnp.int32, (heads, LANES), 0)
    own = lane % heads == sub
    diag = lane == sub
    diag2 = lane == sub + heads

    def look(i, w_ref):
        slot = lax.rem(i, SLOTS)
        s = lax.dot_general(qbuf[i], kbuf[slot], (((1,), (1,)), ((), ())), preferred_element_type=jnp.float32)
        cols = [jnp.where(own, s[:, c : c + LANES], -jnp.inf) for c in range(0, rows, LANES)]
        high = functools.reduce(jnp.maximum, cols)
        high = jnp.max(high, 1, keepdims=True)
        total = jnp.zeros((heads, LANES), jnp.float32)
        for c, col in enumerate(cols):
            w = jnp.exp((col - high) * scale)
            total = total + w
            w_ref[:, c * LANES : (c + 1) * LANES] = w.astype(jnp.bfloat16)
        total = jnp.sum(total, 1, keepdims=True)
        row = jnp.where(diag, high * scale, 0.0) + jnp.where(diag2, total, 0.0)
        stat[i] = jnp.sum(row, 0, keepdims=True)

    def see(i, w_ref):
        slot = lax.rem(i, SLOTS)
        o = jnp.dot(w_ref[...], vbuf[slot], preferred_element_type=jnp.float32)
        part[i] = o.astype(jnp.bfloat16)

    def together(data, stats):
        high = functools.reduce(jnp.maximum, stats)
        f = [jnp.exp(s - high) for s in stats]
        total = functools.reduce(jnp.add, [a * pltpu.roll(s, LANES - heads, 1) for a, s in zip(f, stats)])
        column = lambda r: jnp.sum(jnp.where(diag, jnp.broadcast_to(r, (heads, LANES)), 0.0), 1, keepdims=True)
        seen = functools.reduce(jnp.add, [column(a) * d.astype(jnp.float32) for a, d in zip(f, data)])
        return (seen / column(total)).astype(jnp.bfloat16)

    def rs_copies(i):
        b, owner = i // n, lax.rem(i, n)
        return [
            pltpu.make_async_remote_copy(
                src_ref=src.at[i], dst_ref=dst.at[b, me], send_sem=rs_send.at[x, i], recv_sem=rs_recv.at[x, b, me],
                device_id={AXIS: owner}, device_id_type=MESH,
            )
            for x, (src, dst) in enumerate(((part, rs_data), (stat, rs_stat)))
        ]

    def rs_start(i):
        b, owner = i // n, lax.rem(i, n)

        @pl.when(owner != me)
        def _():
            for c in rs_copies(i):
                c.start()

        @pl.when(owner == me)
        def _():
            rs_data[b, me] = part[i]
            rs_stat[b, me] = stat[i]

    def ag_copy(b, o):
        s, peer = b * n + me, lax.rem(me + o, n)
        return pltpu.make_async_remote_copy(
            src_ref=out.at[s], dst_ref=out.at[s], send_sem=ag_send.at[b, o], recv_sem=ag_recv.at[s],
            device_id={AXIS: peer}, device_id_type=MESH,
        )

    def ag_start(b):
        @pl.when(b * n + me < ringed)
        def _():
            for o in order:
                peer = lax.rem(me + o, n)
                for x, ref in enumerate((rs_data, rs_stat)):
                    pltpu.make_async_remote_copy(
                        src_ref=ref.at[b, peer], dst_ref=ref.at[b, peer], send_sem=rs_send.at[x, 0], recv_sem=rs_recv.at[x, b, peer],
                        device_id={AXIS: peer}, device_id_type=MESH,
                    ).wait_recv()
            out[b * n + me] = together([rs_data[b, d] for d in range(n)], [rs_stat[b, d] for d in range(n)])
            for o in order:
                ag_copy(b, o).start()

    def dr_copies(c, o, peer_slot):
        at, count = starts[c], CHUNKS[c]
        return [
            pltpu.make_async_remote_copy(
                src_ref=src.at[pl.ds(at, count)], dst_ref=dst.at[peer_slot, pl.ds(at - ringed, count)],
                send_sem=dr_send.at[x, c, o], recv_sem=dr_recv.at[x, c, peer_slot],
                device_id={AXIS: lax.rem(me + o, n)}, device_id_type=MESH,
            )
            for x, (src, dst) in enumerate(((part, dr_data), (stat, dr_stat)))
        ]

    def dr_start(c):
        for o in order:
            for copy in dr_copies(c, o, me):
                copy.start()
        for t in range(CHUNKS[c]):
            dr_data[me, starts[c] - ringed + t] = part[starts[c] + t]
            dr_stat[me, starts[c] - ringed + t] = stat[starts[c] + t]

    def dr_end(c):
        for o in order:
            for copy in dr_copies(c, n - o, lax.rem(me + o, n)):
                copy.wait_recv()
        for t in range(CHUNKS[c]):
            at = starts[c] - ringed + t
            out[starts[c] + t] = together([dr_data[d, at] for d in range(n)], [dr_stat[d, at] for d in range(n)])

    q_copy.wait()
    k_copy(0).wait()
    look(0, w0)

    def body(i, w_now, w_next):
        k_copy(i + 1).wait()
        v_copy(i).wait()
        look(i + 1, w_next)
        see(i, w_now)

    batches = -(-ringed // n)
    ag_at = [min((b + 1) * n, ringed) // 2 + 2 for b in range(batches)]

    @pl.loop(0, seqs // 2 - 1)
    def _(p):
        i = 2 * p

        @pl.when(i + SLOTS < seqs)
        def _():
            k_copy(i + SLOTS).start()

        @pl.when(i - 1 + SLOTS < seqs)
        def _():
            v_copy(i - 1 + SLOTS).start()

        body(i, w0, w1)

        @pl.when((i > 0) & (i - 1 < ringed))
        def _():
            rs_start(i - 1)

        @pl.when(i + 1 + SLOTS < seqs)
        def _():
            k_copy(i + 1 + SLOTS).start()

        @pl.when(i + SLOTS < seqs)
        def _():
            v_copy(i + SLOTS).start()

        body(i + 1, w1, w0)

        @pl.when(i < ringed)
        def _():
            rs_start(i)

        for b in range(batches):
            if ag_at[b] < seqs // 2 - 1:

                @pl.when(p == ag_at[b])
                def _():
                    ag_start(b)

    if ringed == seqs - 2:
        rs_start(ringed - 1)
    for c in range(len(CHUNKS)):
        if starts[c] + CHUNKS[c] <= seqs - 2:
            dr_start(c)
    body(seqs - 2, w0, w1)
    for c in range(len(CHUNKS)):
        if starts[c] + CHUNKS[c] == seqs - 1:
            dr_start(c)
    for b in range(batches):
        if ag_at[b] >= seqs // 2 - 1:
            ag_start(b)
    v_copy(seqs - 1).wait()
    see(seqs - 1, w1)
    dr_start(len(CHUNKS) - 1)

    @pl.loop(0, ringed)
    def _(s):
        b, owner = s // n, lax.rem(s, n)

        @pl.when(owner != me)
        def _():
            pltpu.make_async_remote_copy(
                src_ref=out.at[s], dst_ref=out.at[s], send_sem=ag_send.at[b, 0], recv_sem=ag_recv.at[s],
                device_id={AXIS: owner}, device_id_type=MESH,
            ).wait_recv()
            for c in rs_copies(s):
                c.wait_send()

    first = pltpu.make_async_copy(out.at[pl.ds(0, ringed)], o_hbm.at[pl.ds(0, ringed)], osem.at[0])
    first.start()
    for c in range(len(CHUNKS)):
        dr_end(c)
    last = pltpu.make_async_copy(out.at[pl.ds(ringed, direct)], o_hbm.at[pl.ds(ringed, direct)], osem.at[1])
    last.start()
    for b in range(batches):

        @pl.when(b * n + me < ringed)
        def _():
            for o in order:
                ag_copy(b, o).wait_send()

    for c in range(len(CHUNKS)):
        for o in order:
            for copy in dr_copies(c, o, me):
                copy.wait_send()
    first.wait()
    last.wait()


def solution(mesh):
    n = mesh.shape[AXIS]

    def step(q, k, v):
        seqs, tokens, heads, width = k.shape
        rows, direct = tokens * heads, sum(CHUNKS)
        ringed = seqs - direct
        batches, chunks = -(-ringed // n), len(CHUNKS)
        flat = lambda a: a.reshape(seqs, rows, width)
        hbm = pl.BlockSpec(memory_space=pl.ANY)
        dma = pltpu.SemaphoreType.DMA
        return pl.pallas_call(
            functools.partial(kernel, n, seqs, rows, heads, width, width**-0.5),
            out_shape=jax.ShapeDtypeStruct(q.shape, q.dtype),
            in_specs=[hbm] * 3,
            out_specs=hbm,
            scratch_shapes=[
                pltpu.VMEM(q.shape, q.dtype),
                pltpu.VMEM((SLOTS, rows, width), k.dtype),
                pltpu.VMEM((SLOTS, rows, width), v.dtype),
                pltpu.VMEM((heads, rows), jnp.bfloat16),
                pltpu.VMEM((heads, rows), jnp.bfloat16),
                pltpu.VMEM((seqs, heads, width), jnp.bfloat16),
                pltpu.VMEM((seqs, 1, LANES), jnp.float32),
                pltpu.VMEM((seqs, heads, width), jnp.bfloat16),
                pltpu.VMEM((batches, n, heads, width), jnp.bfloat16),
                pltpu.VMEM((batches, n, 1, LANES), jnp.float32),
                pltpu.VMEM((n, direct, heads, width), jnp.bfloat16),
                pltpu.VMEM((n, direct, 1, LANES), jnp.float32),
                dma(()),
                dma((SLOTS,)),
                dma((SLOTS,)),
                dma((2,)),
                dma((2, ringed)),
                dma((2, batches, n)),
                dma((batches, n)),
                dma((ringed,)),
                dma((2, chunks, n)),
                dma((2, chunks, n)),
            ],
            compiler_params=pltpu.CompilerParams(
                collective_id=COLLECTIVE, has_side_effects=True, vmem_limit_bytes=60 * 1024 * 1024
            ),
            cost_estimate=pl.CostEstimate(flops=4 * seqs * rows * width, bytes_accessed=2 * k.size * 2, transcendentals=0),
            name="attend",
        )(q, flat(k), flat(v))

    return jax.shard_map(
        step,
        mesh=mesh,
        in_specs=(P("dp", None, None), P("dp", AXIS, None, None), P("dp", AXIS, None, None)),
        out_specs=P("dp", None, None),
        check_vma=False,
    )
```

time: 151 us -> 60.5 us (0.40)
  matrix products: 64.5 us -> 0 us
  waiting for transfers between devices: 59.6 us -> 0 us
  Pallas kernels: 0 us -> 58.9 us
  between operations: 13.5 us -> 0.01 us
  other arithmetic: 9.95 us -> 0 us
  local copies, waits for them, and re-layouts: 3.6 us -> 1.57 us
    dot_general x2 -> x0, matrix products: 64.5 us -> none  [einsum(): return jnp.einsum(form, a.astype(jnp.float32), b.astype(jnp.float32))]
    all_gather x1 -> x0, waiting for transfers between devices: 59.5 us -> none  [step(): return together(lax.all_gather(part_of(q, k, v), 'sp')).reshape(q.shape)]
    pallas_call x0 -> x1, Pallas kernels: none -> 58.9 us  [step(): pl.pallas_call(functools.partial(kernel, n, seqs, rows, heads, width, wid...]
    reduce_sum x2 -> x0, other arithmetic: 5.68 us -> none  [the longest x1 3 us: together(): jnp.sum(total * scale, 0)]
    mul x1 -> x0, local copies, waits for them, and re-layouts: 3.06 us -> none  [together(): seen * scale]
    reduce_max x2 -> x0, other arithmetic: 2.4 us -> none  [the longest x1 2.27 us: together(): scale = jnp.exp(high - jnp.max(high, 0))]
    unnamed x0 -> x1, local copies, waits for them, and re-layouts: none -> 1.57 us
  transfers between devices with their start and end apart: 1 -> 0, of which waited for: 1 -> 0; matrix products, arithmetic and copies ran while one was open for 0% -> 0% of each run, Pallas kernels for 0% -> 0%
where the time goes in v1:
time: 60.5 us
  Pallas kernels  58.9 us (97%)
  local copies, waits for them, and re-layouts  1.57 us (3%)
    pallas_call x1, Pallas kernels, step(): pl.pallas_call(functools.partial(kernel, n, seqs, rows, heads, width, wid...  58.9 us
    unnamed x1, local copies, waits for them, and re-layouts  1.57 us

profile of v1, /device:TPU:97, one launch (start us, length us, event | category | flops | bytes accessed | tf_op | source)
XLA Modules:
  0.0 60.5 jit_solution(9982831622646913065)
XLA Ops:
  0.0 58.9 %attend.1 = bf16[32,8,256]{2,1,0:T(8,128)(2,1)} custom-call(bf16[32,8,256]{2,1,0:T(8,128)(2,1)} %q_hbm.1, bf16[32,4096,256]{2,1,0:T(8,128)(2,1)} %bitcast.k_hbm, bf16[32,4096,256]{2,1,0:T(8,128)(2,1)} %bitcast.1.v_hbm), custom_call_target="tpu_custom_call" | custom-call | flops 134217728 | bytes 134217728 | tf_op jit(solution)/shard_map/attend/pallas_call | solution.py:277
  58.9 1.6 %copy.5 = bf16[32,8,256]{2,1,0:T(8,128)(2,1)} copy(bf16[32,8,256]{2,1,0:T(8,128)(2,1)} %attend.1) | data formatting | bytes 262144

commit v2 on v1

v2 whole, which is shorter than its diff:
```python
import functools
import math

import jax
import jax.numpy as jnp
from jax import lax
from jax.experimental import pallas as pl
from jax.experimental.pallas import tpu as pltpu
from jax.sharding import PartitionSpec as P

SLOTS = 4
EARLY = 5
TAIL = 4
CHUNKS = (2, 1, 1)
LANES = 128
AXIS = "sp"
MESH = pl.DeviceIdType.MESH
COLLECTIVE = 0


def offsets(n):
    side = math.isqrt(n)
    near = lambda a: min(a, side - a)
    return sorted(range(1, n), key=lambda o: -(near(o // side % side) + near(o % side)))


def kernel(
    n, seqs, rows, heads, width, scale,
    q_hbm, k_hbm, v_hbm, out,
    qbuf, kbuf, vbuf, w0, w1, part, stat,
    rs_data, rs_stat, dr_data, dr_stat,
    qsem, ksem, vsem, tsem,
    rs_send, rs_recv, ag_send, ag_recv, dr_send, dr_recv,
):
    me = lax.axis_index(AXIS)
    direct = sum(CHUNKS)
    ringed = seqs - direct
    starts = [ringed + sum(CHUNKS[:c]) for c in range(len(CHUNKS))]
    order = offsets(n)

    def k_copy(i):
        slot = lax.rem(i, SLOTS)
        return pltpu.make_async_copy(k_hbm.at[i], kbuf.at[slot], ksem.at[slot])

    def v_copy(i):
        slot = lax.rem(i, SLOTS)
        return pltpu.make_async_copy(v_hbm.at[i], vbuf.at[slot], vsem.at[slot])

    def v_piece(t):
        at, slot = pl.ds(t * (rows // TAIL), rows // TAIL), (seqs - 1) % SLOTS
        return pltpu.make_async_copy(v_hbm.at[seqs - 1, at], vbuf.at[slot, at], tsem.at[t])

    def v_start(i):
        @pl.when(i < seqs - 1)
        def _():
            v_copy(i).start()

        @pl.when(i == seqs - 1)
        def _():
            for t in range(TAIL):
                v_piece(t).start()

    q_copy = pltpu.make_async_copy(q_hbm, qbuf, qsem)
    q_copy.start()
    k_copy(0).start()
    for i in range(SLOTS - 1):
        k_copy(i + 1).start()
        v_copy(i).start()

    barrier = pltpu.get_barrier_semaphore()
    for o in order:
        pl.semaphore_signal(barrier, inc=1, device_id={AXIS: lax.rem(me + o, n)}, device_id_type=MESH)

    lane = lax.broadcasted_iota(jnp.int32, (heads, LANES), 1)
    sub = lax.broadcasted_iota(jnp.int32, (heads, LANES), 0)
    own = lane % heads == sub
    diag = lane == sub
    diag2 = lane == sub + heads

    def look(i, w_ref):
        slot = lax.rem(i, SLOTS)
        s = lax.dot_general(qbuf[i], kbuf[slot], (((1,), (1,)), ((), ())), preferred_element_type=jnp.float32)
        cols = [jnp.where(own, s[:, c : c + LANES], -jnp.inf) for c in range(0, rows, LANES)]
        high = functools.reduce(jnp.maximum, cols)
        high = jnp.max(high, 1, keepdims=True)
        total = jnp.zeros((heads, LANES), jnp.float32)
        for c, col in enumerate(cols):
            w = jnp.exp((col - high) * scale)
            total = total + w
            w_ref[:, c * LANES : (c + 1) * LANES] = w.astype(jnp.bfloat16)
        total = jnp.sum(total, 1, keepdims=True)
        row = jnp.where(diag, high * scale, 0.0) + jnp.where(diag2, total, 0.0)
        stat[i] = jnp.sum(row, 0, keepdims=True)

    def see(i, w_ref):
        slot = lax.rem(i, SLOTS)
        o = jnp.dot(w_ref[...], vbuf[slot], preferred_element_type=jnp.float32)
        part[i] = o.astype(jnp.bfloat16)

    def together(data, stats):
        high = functools.reduce(jnp.maximum, stats)
        f = [jnp.exp(s - high) for s in stats]
        total = functools.reduce(jnp.add, [a * pltpu.roll(s, LANES - heads, 1) for a, s in zip(f, stats)])
        column = lambda r: jnp.sum(jnp.where(diag, jnp.broadcast_to(r, (heads, LANES)), 0.0), 1, keepdims=True)
        seen = functools.reduce(jnp.add, [column(a) * d.astype(jnp.float32) for a, d in zip(f, data)])
        return (seen / column(total)).astype(jnp.bfloat16)

    def send(src, dst, send_sem, recv_sem, peer):
        return pltpu.make_async_remote_copy(
            src_ref=src, dst_ref=dst, send_sem=send_sem, recv_sem=recv_sem, device_id={AXIS: peer}, device_id_type=MESH
        )

    other = lax.rem(me + 1, n)

    def arrived(ref, sem):
        send(ref, ref, sem, sem, other).wait_recv()

    def left(ref, sem):
        send(ref, ref, sem, sem, other).wait_send()

    pairs = ((part, rs_data, dr_data), (stat, rs_stat, dr_stat))

    def rs_start(i):
        b, owner = i // n, lax.rem(i, n)

        @pl.when(owner != me)
        def _():
            for x, (src, dst, _) in enumerate(pairs):
                send(src.at[i], dst.at[b, me], rs_send.at[x], rs_recv.at[x, b], owner).start()

        @pl.when(owner == me)
        def _():
            for src, dst, _ in pairs:
                dst[b, me] = src[i]

    def ag_start(b):
        @pl.when(b * n + me < ringed)
        def _():
            for x, (_, ref, _) in enumerate(pairs):
                arrived(ref.at[b, pl.ds(0, n - 1)], rs_recv.at[x, b])
            s = b * n + me
            out[s] = together([rs_data[b, d] for d in range(n)], [rs_stat[b, d] for d in range(n)])
            for o in order:
                send(out.at[s], out.at[s], ag_send.at[b], ag_recv.at[b], lax.rem(me + o, n)).start()

    def dr_start(c):
        at, count = starts[c], CHUNKS[c]
        for o in order:
            for x, (src, _, dst) in enumerate(pairs):
                send(src.at[pl.ds(at, count)], dst.at[me, pl.ds(at - ringed, count)], dr_send.at[x, c], dr_recv.at[x, c], lax.rem(me + o, n)).start()
        for t in range(count):
            for src, _, dst in pairs:
                dst[me, at - ringed + t] = src[at + t]

    def dr_end(c):
        for x, (_, _, ref) in enumerate(pairs):
            arrived(ref.at[pl.ds(0, n - 1), pl.ds(starts[c] - ringed, CHUNKS[c])], dr_recv.at[x, c])
        for t in range(CHUNKS[c]):
            at = starts[c] - ringed + t
            out[starts[c] + t] = together([dr_data[d, at] for d in range(n)], [dr_stat[d, at] for d in range(n)])

    q_copy.wait()
    k_copy(0).wait()
    look(0, w0)

    def body(i, w_now, w_next):
        k_copy(i + 1).wait()
        v_copy(i).wait()
        look(i + 1, w_next)
        see(i, w_now)

    batches = -(-ringed // n)
    ag_at = [min((b + 1) * n, ringed) // 2 + 2 for b in range(batches)]

    def pair(p, send):
        for h, (w_now, w_next) in enumerate(((w0, w1), (w1, w0))):
            i = 2 * p + h

            @pl.when(i + SLOTS < seqs)
            def _():
                k_copy(i + SLOTS).start()

            v_start(i - 1 + SLOTS)
            body(i, w_now, w_next)
            if send:

                @pl.when(i - 1 < ringed)
                def _():
                    rs_start(i - 1)

    @pl.loop(0, EARLY)
    def _(p):
        pair(p, False)

    pl.semaphore_wait(barrier, n - 1)

    @pl.loop(0, 2 * EARLY - 1)
    def _(i):
        rs_start(i)

    @pl.loop(EARLY, seqs // 2 - 1)
    def _(p):
        pair(p, True)

        for b in range(batches):
            if ag_at[b] < seqs // 2 - 1:

                @pl.when(p == ag_at[b])
                def _():
                    ag_start(b)

    if ringed == seqs - 2:
        rs_start(ringed - 1)
    for c in range(len(CHUNKS)):
        if starts[c] + CHUNKS[c] <= seqs - 2:
            dr_start(c)
    body(seqs - 2, w0, w1)
    for c in range(len(CHUNKS)):
        if starts[c] + CHUNKS[c] == seqs - 1:
            dr_start(c)
    for b in range(batches):
        if ag_at[b] >= seqs // 2 - 1:
            ag_start(b)
    slot, step = (seqs - 1) % SLOTS, rows // TAIL
    o = jnp.zeros((heads, width), jnp.float32)
    for t in range(TAIL):
        v_piece(t).wait()
        o = o + jnp.dot(w1[:, t * step : (t + 1) * step], vbuf[slot, t * step : (t + 1) * step], preferred_element_type=jnp.float32)
    part[seqs - 1] = o.astype(jnp.bfloat16)
    dr_start(len(CHUNKS) - 1)

    for b in range(batches):
        here = min(n, ringed - b * n)

        @pl.when(me < here)
        def _():
            arrived(out.at[pl.ds(0, here - 1)], ag_recv.at[b])

        if here < n:

            @pl.when(me >= here)
            def _():
                arrived(out.at[pl.ds(0, here)], ag_recv.at[b])

    for c in range(len(CHUNKS)):
        dr_end(c)

    mine = -(-ringed // n)
    short = ringed % n or n

    @pl.when(me < short)
    def _():
        for x, (src, _, _) in enumerate(pairs):
            left(src.at[pl.ds(0, ringed - mine)], rs_send.at[x])

    if short < n:

        @pl.when(me >= short)
        def _():
            for x, (src, _, _) in enumerate(pairs):
                left(src.at[pl.ds(0, ringed - mine + 1)], rs_send.at[x])

    for b in range(batches):

        @pl.when(b * n + me < ringed)
        def _():
            left(out.at[pl.ds(0, n - 1)], ag_send.at[b])

    for c in range(len(CHUNKS)):
        for x, (_, _, ref) in enumerate(pairs):
            left(ref.at[pl.ds(0, n - 1), pl.ds(starts[c] - ringed, CHUNKS[c])], dr_send.at[x, c])


def solution(mesh):
    n = mesh.shape[AXIS]

    def step(q, k, v):
        seqs, tokens, heads, width = k.shape
        rows, direct = tokens * heads, sum(CHUNKS)
        ringed = seqs - direct
        batches, chunks = -(-ringed // n), len(CHUNKS)
        flat = lambda a: a.reshape(seqs, rows, width)
        dma = pltpu.SemaphoreType.DMA
        return pl.pallas_call(
            functools.partial(kernel, n, seqs, rows, heads, width, width**-0.5),
            out_shape=jax.ShapeDtypeStruct(q.shape, q.dtype),
            in_specs=[pl.BlockSpec(memory_space=pltpu.HBM)] * 3,
            out_specs=pl.BlockSpec(memory_space=pltpu.VMEM),
            scratch_shapes=[
                pltpu.VMEM(q.shape, q.dtype),
                pltpu.VMEM((SLOTS, rows, width), k.dtype),
                pltpu.VMEM((SLOTS, rows, width), v.dtype),
                pltpu.VMEM((heads, rows), jnp.bfloat16),
                pltpu.VMEM((heads, rows), jnp.bfloat16),
                pltpu.VMEM((seqs, heads, width), jnp.bfloat16),
                pltpu.VMEM((seqs, 1, LANES), jnp.float32),
                pltpu.VMEM((batches, n, heads, width), jnp.bfloat16),
                pltpu.VMEM((batches, n, 1, LANES), jnp.float32),
                pltpu.VMEM((n, direct, heads, width), jnp.bfloat16),
                pltpu.VMEM((n, direct, 1, LANES), jnp.float32),
                dma(()),
                dma((SLOTS,)),
                dma((SLOTS,)),
                dma((TAIL,)),
                dma((2,)),
                dma((2, batches)),
                dma((batches,)),
                dma((batches,)),
                dma((2, chunks)),
                dma((2, chunks)),
            ],
            compiler_params=pltpu.CompilerParams(
                collective_id=COLLECTIVE, has_side_effects=True, vmem_limit_bytes=40 * 1024 * 1024
            ),
            cost_estimate=pl.CostEstimate(flops=4 * seqs * rows * width, bytes_accessed=2 * k.size * 2, transcendentals=0),
            name="attend",
        )(q, flat(k), flat(v))

    return jax.shard_map(
        step,
        mesh=mesh,
        in_specs=(P("dp", None, None), P("dp", AXIS, None, None), P("dp", AXIS, None, None)),
        out_specs=P("dp", None, None),
        check_vma=False,
    )
```

time: 60.5 us -> 54.1 us (0.89)
  Pallas kernels: 58.9 us -> 52.4 us
    pallas_call x1, Pallas kernels: 58.9 us -> 52.4 us  [step(): pl.pallas_call(functools.partial(kernel, n, seqs, rows, heads, width, wid...]
    unnamed x1 -> x3, local copies, waits for them, and re-layouts: 1.57 us -> 1.56 us
where the time goes in v2:
time: 54.1 us; the launch traced here: 54 us
  Pallas kernels  52.4 us (97%)
  local copies, waits for them, and re-layouts  1.56 us (3%)
    pallas_call x1, Pallas kernels, step(): pl.pallas_call(functools.partial(kernel, n, seqs, rows, heads, width, wid...  52.4 us
    unnamed x3, local copies, waits for them, and re-layouts  1.56 us

profile of v2, /device:TPU:97, one launch (start us, length us, event | category | flops | bytes accessed | tf_op | source)
XLA Modules:
  0.0 54.0 jit_solution(17535809749452959437)
XLA Ops:
  0.0 0.0 copy-start
  0.0 0.9 %copy-done = bf16[32,8,256]{2,1,0:T(8,128)(2,1)S(1)} copy-done((bf16[32,8,256]{2,1,0:T(8,128)(2,1)S(1)}, bf16[32,8,256]{2,1,0:T(8,128)(2,1)}, u32[]{:S(2)}) %copy-start) | copy-done | bytes 131096
  0.9 52.4 %attend.1 = bf16[32,8,256]{2,1,0:T(8,128)(2,1)S(1)} custom-call(bf16[32,8,256]{2,1,0:T(8,128)(2,1)S(1)} %copy-done, bf16[32,4096,256]{2,1,0:T(8,128)(2,1)} %bitcast.k_hbm, bf16[32,4096,256]{2,1,0:T(8,128)(2,1)} %bitcast.1.v_hbm), custom_call_target="tpu_custom_call" | custom-call | flops 134217728 | bytes 134217728 | tf_op jit(solution)/shard_map/attend/pallas_call | solution.py:284
  53.3 0.7 %copy.5 = bf16[32,8,256]{2,1,0:T(8,128)(2,1)} copy(bf16[32,8,256]{2,1,0:T(8,128)(2,1)S(1)} %attend.1) | data formatting | bytes 262144
Async XLA Ops:
  0.0 0.9 %copy-start = (bf16[32,8,256]{2,1,0:T(8,128)(2,1)S(1)}, bf16[32,8,256]{2,1,0:T(8,128)(2,1)}, u32[]{:S(2)}) copy-start(bf16[32,8,256]{2,1,0:T(8,128)(2,1)} %q_hbm.1) | copy-start | bytes 393220

commit v3 on v2

v3 whole, which is shorter than its diff:
```python
import functools
import math

import jax
import jax.numpy as jnp
from jax import lax
from jax.experimental import pallas as pl
from jax.experimental.pallas import tpu as pltpu
from jax.sharding import PartitionSpec as P

FLIGHT = 3
SLOTS = FLIGHT + 1
AHEAD = 1
LAST = 1
EARLY = 10
TAIL = 2
LATER = 4
CHUNKS = (3, 2)
LANES = 128
AXIS = "sp"
MESH = pl.DeviceIdType.MESH
COLLECTIVE = 0


def offsets(n):
    side = math.isqrt(n)
    near = lambda a: min(a, side - a)
    return sorted(range(1, n), key=lambda o: -(near(o // side % side) + near(o % side)))


def kernel(
    n, seqs, rows, heads, width, scale,
    q_hbm, k_hbm, v_hbm, out,
    qbuf, kbuf, vbuf, wbuf, part, stat,
    rs_data, rs_stat, dr_data, dr_stat,
    qsem, ksem, vsem, tsem,
    rs_send, rs_recv, ag_send, ag_recv, dr_send, dr_recv, st_sem,
):
    me = lax.axis_index(AXIS)
    direct = sum(CHUNKS)
    ringed = seqs - direct
    starts = [ringed + sum(CHUNKS[:c]) for c in range(len(CHUNKS))]
    order = offsets(n)

    def k_copy(i):
        slot = lax.rem(i, SLOTS)
        return pltpu.make_async_copy(k_hbm.at[i], kbuf.at[slot], ksem.at[slot])

    def v_copy(i):
        slot = lax.rem(i, SLOTS)
        return pltpu.make_async_copy(v_hbm.at[i], vbuf.at[slot], vsem.at[slot])

    def v_piece(t):
        at, slot = pl.ds(t * (rows // TAIL), rows // TAIL), (seqs - 1) % SLOTS
        return pltpu.make_async_copy(v_hbm.at[seqs - 1, at], vbuf.at[slot, at], tsem.at[t])

    def k_piece(t):
        at = pl.ds(t * (rows // TAIL), rows // TAIL)
        return pltpu.make_async_copy(k_hbm.at[0, at], kbuf.at[0, at], tsem.at[t])

    def k_start(i):
        @pl.when(i < seqs)
        def _():
            k_copy(i).start()

    def v_start(i):
        @pl.when(i < seqs - 1)
        def _():
            v_copy(i).start()

        @pl.when(i == seqs - 1)
        def _():
            for t in range(TAIL):
                v_piece(t).start()

    q_copy = pltpu.make_async_copy(q_hbm, qbuf, qsem)
    q_copy.start()
    for t in range(TAIL):
        k_piece(t).start()
    for i in range(1, FLIGHT):
        k_start(i)
    for i in range(FLIGHT):
        v_start(i)

    barrier = pltpu.get_barrier_semaphore()
    for o in order:
        pl.semaphore_signal(barrier, inc=1, device_id={AXIS: lax.rem(me + o, n)}, device_id_type=MESH)

    lane = lax.broadcasted_iota(jnp.int32, (heads, LANES), 1)
    sub = lax.broadcasted_iota(jnp.int32, (heads, LANES), 0)
    own = lane % heads == sub
    diag = lane == sub
    diag2 = lane == sub + heads

    def look(i):
        i = jnp.int32(i)
        slot, w = lax.rem(i, SLOTS), lax.rem(i, AHEAD + 1)
        s = lax.dot_general(qbuf[i], kbuf[slot], (((1,), (1,)), ((), ())), preferred_element_type=jnp.float32)
        cols = [jnp.where(own, s[:, c : c + LANES], -jnp.inf) for c in range(0, rows, LANES)]
        high = jnp.max(functools.reduce(jnp.maximum, cols), 1, keepdims=True)
        total = jnp.zeros((heads, LANES), jnp.float32)
        for c, col in enumerate(cols):
            e = jnp.exp((col - high) * scale)
            total = total + e
            wbuf[w, :, c * LANES : (c + 1) * LANES] = e.astype(jnp.bfloat16)
        total = jnp.sum(total, 1, keepdims=True)
        row = jnp.where(diag, high * scale, 0.0) + jnp.where(diag2, total, 0.0)
        stat[i] = jnp.sum(row, 0, keepdims=True)

    def see(i):
        slot, w = lax.rem(i, SLOTS), lax.rem(i, AHEAD + 1)
        o = jnp.dot(wbuf[w], vbuf[slot], preferred_element_type=jnp.float32)
        part[i] = o.astype(jnp.bfloat16)

    def shares(stats):
        high = functools.reduce(jnp.maximum, stats)
        f = [jnp.exp(s - high) for s in stats]
        total = functools.reduce(jnp.add, [a * pltpu.roll(s, LANES - heads, 1) for a, s in zip(f, stats)])
        column = lambda r: jnp.sum(jnp.where(diag, jnp.broadcast_to(r, (heads, LANES)), 0.0), 1, keepdims=True)
        return [column(a) for a in f], column(total)

    def together(data, counts):
        f, total = counts
        seen = functools.reduce(jnp.add, [a * d.astype(jnp.float32) for a, d in zip(f, data)])
        return (seen / total).astype(jnp.bfloat16)

    def send(src, dst, send_sem, recv_sem, peer):
        return pltpu.make_async_remote_copy(
            src_ref=src, dst_ref=dst, send_sem=send_sem, recv_sem=recv_sem, device_id={AXIS: peer}, device_id_type=MESH
        )

    other = lax.rem(me + 1, n)

    def arrived(ref, sem):
        send(ref, ref, sem, sem, other).wait_recv()

    def left(ref, sem):
        send(ref, ref, sem, sem, other).wait_send()

    pairs = ((part, rs_data), (stat, rs_stat))

    def rs_start(i):
        b, owner = i // n, lax.rem(i, n)

        @pl.when(owner != me)
        def _():
            for x, (src, dst) in enumerate(pairs):
                send(src.at[i], dst.at[b, me], rs_send.at[x], rs_recv.at[x, b], owner).start()

        @pl.when(owner == me)
        def _():
            for src, dst in pairs:
                dst[b, me] = src[i]

    def ag_start(b):
        @pl.when(b * n + me < ringed)
        def _():
            for x, (_, ref) in enumerate(pairs):
                arrived(ref.at[b, pl.ds(0, n - 1)], rs_recv.at[x, b])
            s = b * n + me
            out[s] = together([rs_data[b, d] for d in range(n)], shares([rs_stat[b, d] for d in range(n)]))
            for o in order:
                send(out.at[s], out.at[s], ag_send.at[b], ag_recv.at[b], lax.rem(me + o, n)).start()

    tops = pl.ds(ringed, direct)

    def tops_start():
        for t in range(direct):
            dr_stat[me, t] = stat[ringed + t]
        for o in order:
            send(stat.at[tops], dr_stat.at[me], st_sem.at[0], st_sem.at[1], lax.rem(me + o, n)).start()

    def dr_start(c):
        at, count = starts[c], CHUNKS[c]
        for t in range(count):
            dr_data[me, at - ringed + t] = part[at + t]
        for o in order:
            send(part.at[pl.ds(at, count)], dr_data.at[me, pl.ds(at - ringed, count)], dr_send.at[c], dr_recv.at[c], lax.rem(me + o, n)).start()

    def dr_end(c):
        at, count = starts[c] - ringed, CHUNKS[c]
        counts = [shares([dr_stat[d, at + t] for d in range(n)]) for t in range(count)]
        arrived(dr_data.at[pl.ds(0, n - 1), pl.ds(at, count)], dr_recv.at[c])
        for t in range(count):
            out[starts[c] + t] = together([dr_data[d, at + t] for d in range(n)], counts[t])

    batches = -(-ringed // n)
    ag_at = [min((b + 1) * n, ringed) - 1 + LATER for b in range(batches)]
    steady = seqs - AHEAD - LAST

    q_copy.wait()
    for t in range(TAIL):
        k_piece(t).wait()
    k_start(FLIGHT)
    look(0)

    @pl.loop(1, AHEAD)
    def _(i):
        k_copy(i).wait()
        k_start(i + FLIGHT)
        look(i)

    def body(i):
        k_copy(i + AHEAD).wait()
        k_start(i + AHEAD + FLIGHT)
        v_copy(i).wait()
        v_start(i + FLIGHT)
        see(i)
        look(i + AHEAD)

    @pl.loop(0, EARLY)
    def _(i):
        body(i)

    pl.semaphore_wait(barrier, n - 1)

    @pl.loop(0, EARLY - 1)
    def _(i):
        rs_start(i)

    @pl.loop(EARLY, steady)
    def _(i):
        body(i)

        @pl.when(i - 1 < ringed)
        def _():
            rs_start(i - 1)

        for b in range(batches):
            if ag_at[b] < steady:

                @pl.when(i == ag_at[b])
                def _():
                    ag_start(b)

        for c in range(len(CHUNKS)):
            if starts[c] + CHUNKS[c] - 1 < steady:

                @pl.when(i == starts[c] + CHUNKS[c] - 1)
                def _():
                    dr_start(c)

    def after(i):
        if i - 1 < ringed:
            rs_start(i - 1)
        for c in range(len(CHUNKS)):
            if starts[c] + CHUNKS[c] - 1 == i:
                dr_start(c)
        for b in range(batches):
            if ag_at[b] == i:
                ag_start(b)

    for i in range(steady, seqs - 1):
        if i + AHEAD < seqs:
            k_copy(i + AHEAD).wait()
            k_start(i + AHEAD + FLIGHT)
            look(i + AHEAD)
        if i + AHEAD == seqs - 1:
            tops_start()
        v_copy(i).wait()
        v_start(i + FLIGHT)
        see(i)
        after(i)

    slot, step = (seqs - 1) % SLOTS, rows // TAIL
    w = (seqs - 1) % (AHEAD + 1)
    o = jnp.zeros((heads, width), jnp.float32)
    for t in range(TAIL):
        v_piece(t).wait()
        at = slice(t * step, (t + 1) * step)
        o = o + jnp.dot(wbuf[w, :, at], vbuf[slot, at], preferred_element_type=jnp.float32)
    part[seqs - 1] = o.astype(jnp.bfloat16)
    after(seqs - 1)

    for b in range(batches):
        here = min(n, ringed - b * n)

        @pl.when(me < here)
        def _():
            arrived(out.at[pl.ds(0, here - 1)], ag_recv.at[b])

        if here < n:

            @pl.when(me >= here)
            def _():
                arrived(out.at[pl.ds(0, here)], ag_recv.at[b])

    arrived(dr_stat.at[pl.ds(0, n - 1)], st_sem.at[1])
    for c in range(len(CHUNKS)):
        dr_end(c)

    mine = -(-ringed // n)
    short = ringed % n or n

    @pl.when(me < short)
    def _():
        for x, (src, _) in enumerate(pairs):
            left(src.at[pl.ds(0, ringed - mine)], rs_send.at[x])

    if short < n:

        @pl.when(me >= short)
        def _():
            for x, (src, _) in enumerate(pairs):
                left(src.at[pl.ds(0, ringed - mine + 1)], rs_send.at[x])

    for b in range(batches):

        @pl.when(b * n + me < ringed)
        def _():
            left(out.at[pl.ds(0, n - 1)], ag_send.at[b])

    for c in range(len(CHUNKS)):
        left(dr_data.at[pl.ds(0, n - 1), pl.ds(starts[c] - ringed, CHUNKS[c])], dr_send.at[c])
    left(dr_stat.at[pl.ds(0, n - 1)], st_sem.at[0])


def solution(mesh):
    n = mesh.shape[AXIS]

    def step(q, k, v):
        seqs, tokens, heads, width = k.shape
        rows, direct = tokens * heads, sum(CHUNKS)
        ringed = seqs - direct
        batches, chunks = -(-ringed // n), len(CHUNKS)
        flat = lambda a: a.reshape(seqs, rows, width)
        dma = pltpu.SemaphoreType.DMA
        return pl.pallas_call(
            functools.partial(kernel, n, seqs, rows, heads, width, width**-0.5),
            out_shape=jax.ShapeDtypeStruct(q.shape, q.dtype),
            in_specs=[pl.BlockSpec(memory_space=pltpu.HBM)] * 3,
            out_specs=pl.BlockSpec(memory_space=pltpu.VMEM),
            scratch_shapes=[
                pltpu.VMEM(q.shape, q.dtype),
                pltpu.VMEM((SLOTS, rows, width), k.dtype),
                pltpu.VMEM((SLOTS, rows, width), v.dtype),
                pltpu.VMEM((AHEAD + 1, heads, rows), jnp.bfloat16),
                pltpu.VMEM((seqs, heads, width), jnp.bfloat16),
                pltpu.VMEM((seqs, 1, LANES), jnp.float32),
                pltpu.VMEM((batches, n, heads, width), jnp.bfloat16),
                pltpu.VMEM((batches, n, 1, LANES), jnp.float32),
                pltpu.VMEM((n, direct, heads, width), jnp.bfloat16),
                pltpu.VMEM((n, direct, 1, LANES), jnp.float32),
                dma(()),
                dma((SLOTS,)),
                dma((SLOTS,)),
                dma((TAIL,)),
                dma((2,)),
                dma((2, batches)),
                dma((batches,)),
                dma((batches,)),
                dma((chunks,)),
                dma((chunks,)),
                dma((2,)),
            ],
            compiler_params=pltpu.CompilerParams(
                collective_id=COLLECTIVE, has_side_effects=True, vmem_limit_bytes=40 * 1024 * 1024
            ),
            cost_estimate=pl.CostEstimate(flops=4 * seqs * rows * width, bytes_accessed=2 * k.size * 2, transcendentals=0),
            name="attend",
        )(pltpu.with_memory_space_constraint(q, pltpu.HBM), flat(k), flat(v))

    return jax.shard_map(
        step,
        mesh=mesh,
        in_specs=(P("dp", None, None), P("dp", AXIS, None, None), P("dp", AXIS, None, None)),
        out_specs=P("dp", None, None),
        check_vma=False,
    )
```

time: 54.1 us -> 52.5 us (0.970)
  local copies, waits for them, and re-layouts: 1.56 us -> 0.66 us
  Pallas kernels: 52.4 us -> 51.8 us
    unnamed x3 -> x1, local copies, waits for them, and re-layouts: 1.56 us -> 0.66 us
    pallas_call x1, Pallas kernels: 52.4 us -> 51.8 us  [step(): pl.pallas_call(functools.partial(kernel, n, seqs, rows, heads, width, wid...]
where the time goes in v3:
time: 52.5 us; the launch traced here: 52.4 us
  Pallas kernels  51.8 us (99%)
  local copies, waits for them, and re-layouts  0.66 us (1%)
    pallas_call x1, Pallas kernels, step(): pl.pallas_call(functools.partial(kernel, n, seqs, rows, heads, width, wid...  51.8 us

profile of v3, /device:TPU:97, one launch (start us, length us, event | category | flops | bytes accessed | tf_op | source)
XLA Modules:
  0.0 52.4 jit_solution(16199336631485976650)
XLA Ops:
  0.0 51.8 %attend.1 = bf16[32,8,256]{2,1,0:T(8,128)(2,1)S(1)} custom-call(bf16[32,8,256]{2,1,0:T(8,128)(2,1)} %q_hbm.1, bf16[32,4096,256]{2,1,0:T(8,128)(2,1)} %bitcast.k_hbm, bf16[32,4096,256]{2,1,0:T(8,128)(2,1)} %bitcast.1.v_hbm), custom_call_target="tpu_custom_call" | custom-call | flops 134217728 | bytes 134217728 | tf_op jit(solution)/shard_map/attend/pallas_call | solution.py:328
  51.8 0.7 %copy.5 = bf16[32,8,256]{2,1,0:T(8,128)(2,1)} copy(bf16[32,8,256]{2,1,0:T(8,128)(2,1)S(1)} %attend.1) | data formatting | bytes 262144

commit v4 on v3

--- a/solution.py
+++ b/solution.py
@@ -13,7 +13,7 @@
 AHEAD = 1
 LAST = 1
 EARLY = 10
-TAIL = 2
+TAIL = 1
 LATER = 4
 CHUNKS = (3, 2)
 LANES = 128
@@ -25,7 +25,8 @@
 def offsets(n):
     side = math.isqrt(n)
     near = lambda a: min(a, side - a)
-    return sorted(range(1, n), key=lambda o: -(near(o // side % side) + near(o % side)))
+    steps = [(a, b) for a in range(side) for b in range(side) if a or b]
+    return sorted(steps, key=lambda s: -(near(s[0]) + near(s[1])))
 
 
 def kernel(
@@ -40,7 +41,8 @@
     direct = sum(CHUNKS)
     ringed = seqs - direct
     starts = [ringed + sum(CHUNKS[:c]) for c in range(len(CHUNKS))]
-    order = offsets(n)
+    order, side = offsets(n), math.isqrt(n)
+    peer = lambda o: lax.rem(me // side + o[0], side) * side + lax.rem(me + o[1], side)
 
     def k_copy(i):
         slot = lax.rem(i, SLOTS)
@@ -79,12 +81,12 @@
         k_piece(t).start()
     for i in range(1, FLIGHT):
         k_start(i)
-    for i in range(FLIGHT):
+    for i in range(FLIGHT - 1):
         v_start(i)
 
     barrier = pltpu.get_barrier_semaphore()
     for o in order:
-        pl.semaphore_signal(barrier, inc=1, device_id={AXIS: lax.rem(me + o, n)}, device_id_type=MESH)
+        pl.semaphore_signal(barrier, inc=1, device_id={AXIS: peer(o)}, device_id_type=MESH)
 
     lane = lax.broadcasted_iota(jnp.int32, (heads, LANES), 1)
     sub = lax.broadcasted_iota(jnp.int32, (heads, LANES), 0)
@@ -160,7 +162,7 @@
             s = b * n + me
             out[s] = together([rs_data[b, d] for d in range(n)], shares([rs_stat[b, d] for d in range(n)]))
             for o in order:
-                send(out.at[s], out.at[s], ag_send.at[b], ag_recv.at[b], lax.rem(me + o, n)).start()
+                send(out.at[s], out.at[s], ag_send.at[b], ag_recv.at[b], peer(o)).start()
 
     tops = pl.ds(ringed, direct)
 
@@ -168,14 +170,14 @@
         for t in range(direct):
             dr_stat[me, t] = stat[ringed + t]
         for o in order:
-            send(stat.at[tops], dr_stat.at[me], st_sem.at[0], st_sem.at[1], lax.rem(me + o, n)).start()
+            send(stat.at[tops], dr_stat.at[me], st_sem.at[0], st_sem.at[1], peer(o)).start()
 
     def dr_start(c):
         at, count = starts[c], CHUNKS[c]
         for t in range(count):
             dr_data[me, at - ringed + t] = part[at + t]
         for o in order:
-            send(part.at[pl.ds(at, count)], dr_data.at[me, pl.ds(at - ringed, count)], dr_send.at[c], dr_recv.at[c], lax.rem(me + o, n)).start()
+            send(part.at[pl.ds(at, count)], dr_data.at[me, pl.ds(at - ringed, count)], dr_send.at[c], dr_recv.at[c], peer(o)).start()
 
     def dr_end(c):
         at, count = starts[c] - ringed, CHUNKS[c]
@@ -192,6 +194,7 @@
     for t in range(TAIL):
         k_piece(t).wait()
     k_start(FLIGHT)
+    v_start(FLIGHT - 1)
     look(0)
 
     @pl.loop(1, AHEAD)

time: 52.5 us -> 52.4 us (level)
  no operation moved by 1% of the time
where the time goes in v4:
time: 52.4 us; the launch traced here: 52.3 us
  Pallas kernels  51.6 us (98%)
  local copies, waits for them, and re-layouts  0.66 us (1%)
    pallas_call x1, Pallas kernels, step(): pl.pallas_call(functools.partial(kernel, n, seqs, rows, heads, width, wid...  51.6 us

profile of v4, /device:TPU:97, one launch (start us, length us, event | category | flops | bytes accessed | tf_op | source)
XLA Modules:
  0.0 52.3 jit_solution(15510918734596821810)
XLA Ops:
  0.0 51.6 %attend.1 = bf16[32,8,256]{2,1,0:T(8,128)(2,1)S(1)} custom-call(bf16[32,8,256]{2,1,0:T(8,128)(2,1)} %q_hbm.1, bf16[32,4096,256]{2,1,0:T(8,128)(2,1)} %bitcast.k_hbm, bf16[32,4096,256]{2,1,0:T(8,128)(2,1)} %bitcast.1.v_hbm), custom_call_target="tpu_custom_call" | custom-call | flops 134217728 | bytes 134217728 | tf_op jit(solution)/shard_map/attend/pallas_call | solution.py:331
  51.6 0.7 %copy.5 = bf16[32,8,256]{2,1,0:T(8,128)(2,1)} copy(bf16[32,8,256]{2,1,0:T(8,128)(2,1)S(1)} %attend.1) | data formatting | bytes 262144
